TPU v7x, 32 devices: a whole 2x2x4 slice. The times are simulated.
32 devices in a mesh: cell: 16 (over z, y, x), pre: 2 (over core).
Axes of the slice: x: 2, y: 2, z: 4, core: 2. Of those that a mesh axis runs over, the one named last changes fastest.
Arguments:
- v_init: float32 [128, 16, 4096], P(None, None, ('cell', 'pre')), may hold values from -6 to 6
- cotangent: float32 [128, 16, 4096], P(None, None, ('cell', 'pre')), may hold values from -6 to 6
- weights: bfloat16 [4096, 4096], P('cell', 'pre'), may hold values from -2 to 2
- leak: float32 [4096], P(('cell', 'pre')), may hold values from 0.2 to 1.5
- drive: float32 [4096], P(('cell', 'pre')), may hold values from 0.5 to 2
- site: int32 [4096], P(('cell', 'pre')), may hold values from 0 to 127
- parent: int32 [128], replicated, may hold values from 0 to 126, as said below
- axial: float32 [128], replicated, may hold values from 1 to 8
- cap: float32 [128], replicated, may hold values from 2 to 6
- bank: float32 [16, 128], replicated, may hold values from -5 to 5
- sched: int32 [2, 16], replicated, may hold values from 0 to 15
Outputs:
- v_final: float32 [128, 16, 4096], P(None, None, ('cell', 'pre'))
- v_grad: float32 [128, 16, 4096], P(None, None, ('cell', 'pre'))
Inputs may be any that keep to these rules, and one draw needn't show every extreme that they name: parent[0] = 0, and for i >= 1 parent[i] < i and i - parent[i] <= 8.
All inputs are finite; a program needn't handle non-finite values.
Results may differ from a plain program's by a relative error of at most 0.0021.
Values may be sent and summed in bfloat16 or wider, within the bound.
A program may use at most 64 MiB of HBM per device.

v0:
```python
import jax
import jax.numpy as jnp
from jax import lax
from jax.sharding import PartitionSpec as P

reversal = 1.0


def tree_inverse(parent, axial, cap):
    length = parent.shape[0]
    indices = jnp.arange(length, dtype=jnp.int32)
    onehot = (parent[:, None] == indices[None, :]).astype(jnp.float32)
    ident = jnp.eye(length, dtype=jnp.float32)
    edges = (ident - onehot) * (indices > 0).astype(jnp.float32)[:, None]
    shunt = axial * (indices == 0).astype(jnp.float32)
    system = jnp.diag(cap + shunt) + jnp.dot(
        edges.T * axial[None, :], edges, precision=lax.Precision.HIGHEST
    )
    lower = jnp.linalg.cholesky(system)
    factor = lax.linalg.triangular_solve(lower, ident, left_side=True, lower=True)
    return jnp.dot(factor.T, factor, precision=lax.Precision.HIGHEST)


def apply_matrix(matrix, field):
    depth, trials, cells = field.shape
    flat = jnp.dot(matrix, field.reshape(depth, trials * cells), precision=lax.Precision.HIGHEST)
    return flat.reshape(depth, trials, cells)


def forward_drive(activity, weights):
    partial_rows = lax.dot_general(
        lax.all_gather(activity, "cell", axis=1, tiled=True),
        weights,
        (((1,), (1,)), ((), ())),
        preferred_element_type=jnp.float32,
    )
    return lax.psum_scatter(partial_rows, "pre", scatter_dimension=1, tiled=True)


def backward_drive(site_adjoint, weights):
    partial_cols = jnp.dot(
        lax.all_gather(site_adjoint, "pre", axis=1, tiled=True),
        weights,
        preferred_element_type=jnp.float32,
    )
    return lax.psum_scatter(partial_cols, "cell", scatter_dimension=1, tiled=True)


def body(v_init, cotangent, weights, leak, drive, site, parent, axial, cap, bank, sched):
    inverse = tree_inverse(parent, axial, cap)
    depth = parent.shape[0]
    comps = jnp.arange(depth, dtype=jnp.int32)
    mask = (site[None, :] == comps[:, None]).astype(jnp.float32)
    levels = cap[:, None, None] - leak[None, None, :]
    select = (
        sched[:, :, None] == jnp.arange(bank.shape[0], dtype=jnp.int32)[None, None, :]
    ).astype(jnp.float32)
    field = v_init
    saved = []
    for moment in range(sched.shape[0]):
        rates = jax.nn.sigmoid(field[0])
        activity = rates.astype(jnp.bfloat16)
        synaptic = forward_drive(activity, weights)
        pattern = jnp.dot(select[moment], bank, precision=lax.Precision.HIGHEST)
        source = pattern.T[:, :, None] * drive[None, None, :]
        total = levels * field + mask[:, None, :] * synaptic[None] * (reversal - field) + source
        saved.append((field, rates, synaptic))
        field = apply_matrix(inverse, total)
    adjoint = cotangent
    for moment in range(sched.shape[0] - 1, -1, -1):
        state, rates, synaptic = saved[moment]
        pulled = apply_matrix(inverse.T, adjoint)
        site_adjoint = jnp.sum(mask[:, None, :] * pulled * (reversal - state), axis=0).astype(
            jnp.bfloat16
        )
        returned = backward_drive(site_adjoint, weights)
        adjoint = levels * pulled - mask[:, None, :] * synaptic[None] * pulled
        adjoint = adjoint.at[0].add(returned * rates * (1.0 - rates))
    return (field, adjoint)


def solution(mesh):
    in_specs = (
        P(None, None, ("cell", "pre")),
        P(None, None, ("cell", "pre")),
        P("cell", "pre"),
        P(("cell", "pre")),
        P(("cell", "pre")),
        P(("cell", "pre")),
        P(),
        P(),
        P(),
        P(),
        P(),
    )
    out_specs = (P(None, None, ("cell", "pre")), P(None, None, ("cell", "pre")))
    return jax.shard_map(body, mesh=mesh, in_specs=in_specs, out_specs=out_specs, check_vma=False)
```

profile of v0, /device:TPU:0, one launch (start us, length us, event | category | flops | bytes accessed | tf_op | source)
XLA Modules:
  0.0 310.3 jit_solution(1017453609851802560)
XLA Ops:
  7.2 0.8 bitcast_convert_fusion
  8.0 42.7 %all_gather.12 = bf16[16,2048]{1,0:T(8,128)(2,1)S(1)} all-gather(bf16[16,128]{1,0:T(8,128)(2,1)S(1)} %bitcast_convert_fusion), channel_id=1, replica_groups=mesh['cell'=16,'pre'=2] {'cell'}, dimensions={1}, use_global_device_ids=true | all-gather | bytes 69632 | tf_op jit(solution)/shard_map/all_gather | solution.py:32
  50.8 1.0 fusion.42
  53.8 0.6 copy-done.10
  55.6 11.7 %cholesky.18 = f32[128,128]{1,0:T(8,128)S(1)} custom-call(f32[128,128]{1,0:T(8,128)S(1)} %fusion.18), custom_call_target="Cholesky" | custom-call | tf_op jit(solution)/shard_map/jit(cholesky)/cholesky | solution.py:19
  68.0 0.7 fusion.8
  68.6 9.8 %custom-call.6 = f32[1,128,128]{1,2,0:T(8,128)S(1)} custom-call(f32[1,128,128]{2,1,0:T(8,128)S(1)} %fusion.8), custom_call_target="InvertDiagBlocksLowerTriangular" | custom-call | tf_op jit(solution)/shard_map/triangular_solve | solution.py:20
  80.2 1.1 fusion.1
  81.3 1.3 copy.35
  82.6 2.2 fusion.43
  84.9 35.8 %all_gather.13 = bf16[16,2048]{1,0:T(8,128)(2,1)S(1)} all-gather(bf16[16,128]{1,0:T(8,128)(2,1)S(1)} %convert_element_type.49), channel_id=1, replica_groups=mesh['cell'=16,'pre'=2] {'cell'}, dimensions={1}, use_global_device_ids=true | all-gather | bytes 69632 | tf_op jit(solution)/shard_map/all_gather | solution.py:32
  120.7 1.0 fusion.44
  122.1 2.5 copy.77
  124.6 2.6 copy.39
  128.3 2.9 subtract_bitcast_fusion
  131.2 2.6 copy.52
  133.8 3.3 %fusion.7 = (bf16[16,128]{1,0:T(8,128)(2,1)S(1)}, f32[128,16,128]{2,0,1:T(8,128)}) fusion(f32[16,16,8,128]{3,2,1,0:T(8,128)} %get-tuple-element.32, f32[128,128]{1,0:T(8,128)S(1)} %fusion.29, f32[16,128,128]{2,1,0:T(8,128)S(1)} %bitcast.115, f32[128,128]{1,0:T(8,128)S(1)} %fusion.41), kind=kOutput, calls=%fused_computation.17 | convolution fusion | flops 403437568 | bytes 3280896 | tf_op jit(solution)/shard_map/dot_general | solution.py:26
  137.1 1.8 all_gather.14
  139.0 0.9 fusion.45
  140.0 1.9 multiply_subtract_fusion
  141.9 76.3 %reduce-scatter.9.cloned.1.call-done = f32[16,128]{1,0:T(8,128)} async-done(((f32[16,2048]{1,0:T(8,128)}), f32[16,128]{1,0:T(8,128)}) %reduce-scatter.9.cloned.1.call-update) | async-done | bytes 8208 | tf_op jit(solution)/shard_map/reduce_scatter | solution.py:46
  218.2 0.7 fusion.35
  218.9 1.3 copy.76
  220.2 2.5 copy.46
  222.7 2.6 multiply_reduce_fusion
  225.4 1.8 all_gather.15
  227.2 0.9 fusion.46
  228.2 2.2 fusion.13
  230.4 1.6 copy.48
  232.0 69.4 %reduce-scatter.11.cloned.1.call-done = f32[16,128]{1,0:T(8,128)} async-done(((f32[16,2048]{1,0:T(8,128)}), f32[16,128]{1,0:T(8,128)}) %reduce-scatter.11.cloned.1.call-update) | async-done | bytes 8208 | tf_op jit(solution)/shard_map/reduce_scatter | solution.py:46
  301.4 0.7 fusion.39
  302.2 1.6 copy.49
  (58 shorter events, 7.2 us)
Async XLA Ops:
  7.2 43.6 %copy-start = (bf16[256,2048]{1,0:T(8,128)(2,1)S(1)}, bf16[256,2048]{1,0:T(8,128)(2,1)}, u32[]{:S(2)}) copy-start(bf16[256,2048]{1,0:T(8,128)(2,1)} %param.17) | copy-start | bytes 3145732
  7.2 72.5 %reduce-scatter.5.cloned.1.call-start = ((), (), s32[]{:S(2)}) async-start(), calls=%async_computation.4 | async-start | bytes 24576 | tf_op jit(solution)/shard_map/reduce_scatter | solution.py:37
  50.8 28.9 %copy-start.1 = (f32[128,16,128]{2,1,0:T(8,128)S(1)}, f32[128,16,128]{2,1,0:T(8,128)}, u32[]{:S(2)}) copy-start(f32[128,16,128]{2,1,0:T(8,128)} %param.15) | copy-start | bytes 3145732
  51.8 0.7 copy-start.7
  51.8 75.4 %reduce-scatter.7.cloned.1.call-start = ((), (), s32[]{:S(2)}) async-start(), calls=%async_computation.5 | async-start | bytes 24576 | tf_op jit(solution)/shard_map/reduce_scatter | solution.py:37
  52.5 0.7 copy-start.8
  53.1 0.7 copy-start.9
  53.1 0.7 copy-start.12
  53.8 0.7 copy-start.10
  54.4 0.7 copy-start.11
  78.7 0.7 copy-start.5
  79.5 0.7 copy-start.6
  121.7 96.4 %reduce-scatter.9.cloned.1.call-start = ((), (), s32[]{:S(2)}) async-start(), calls=%async_computation.6 | async-start | bytes 139264 | tf_op jit(solution)/shard_map/reduce_scatter | solution.py:46
  127.6 0.7 copy-start.4
  131.2 2.6 copy-start.2
  139.9 161.5 %reduce-scatter.11.cloned.1.call-start = ((), (), s32[]{:S(2)}) async-start(), calls=%async_computation.7 | async-start | bytes 139264 | tf_op jit(solution)/shard_map/reduce_scatter | solution.py:46
  220.2 2.5 copy-start.3
Sparse Core Ops, SparseCore 0:
  51.9 3.4 reduce-scatter.4
  121.9 5.2 reduce-scatter.6
  140.0 78.0 reduce-scatter.8
  228.3 73.1 reduce-scatter.10
where the time goes:
time: 311 us; the launch traced here: 310 us
  waiting for transfers between devices  146 us (47%)
  blocking collectives  82.2 us (26%)
  other arithmetic  31.3 us (10%)
  local copies, waits for them, and re-layouts  21.4 us (7%)
  matrix products  15.3 us (5%)
  between operations  14 us (5%)
    reduce_scatter x2, waiting for transfers between devices, backward_drive(): lax.psum_scatter(partial_cols, 'cell', scatter_dimension=1, tiled=True)  146 us
    all_gather x2, blocking collectives, forward_drive(): lax.all_gather(activity, 'cell', axis=1, tiled=True)  78.5 us
    another operation x3, other arithmetic, tree_inverse(): lower = jnp.linalg.cholesky(system)  12.4 us
    unnamed x30, local copies, waits for them, and re-layouts  11.7 us
    another operation x2, other arithmetic, tree_inverse(): lax.linalg.triangular_solve(lower, ident, left_side=True, lower=True)  10.5 us
    dot_general x4, matrix products, apply_matrix(): jnp.dot(matrix, field.reshape(depth, trials * cells), precision=lax.Preci...  10.4 us
    dot_general x3, local copies, waits for them, and re-layouts, apply_matrix(): jnp.dot(matrix, field.reshape(depth, trials * cells), precision=lax.Preci...  7.73 us
  transfers between devices with their start and end apart: 4, of which 2 were waited for; matrix products, arithmetic and copies ran while one was open for 11% of the time, Pallas kernels for 0%

commit v1 on v0

--- a/solution.py
+++ b/solution.py
@@ -29,7 +29,9 @@
 
 def forward_drive(activity, weights):
     partial_rows = lax.dot_general(
-        lax.all_gather(activity, "cell", axis=1, tiled=True),
+        jnp.concatenate(
+            lax.all_to_all(jnp.stack([activity] * lax.axis_size("cell")), "cell", 0, 0), axis=1
+        ),
         weights,
         (((1,), (1,)), ((), ())),
         preferred_element_type=jnp.float32,

time: 311 us -> 263 us (0.85)
  blocking collectives: 82.2 us -> 3.67 us
  starting transfers between devices: 0.34 us -> 15.4 us
  waiting for transfers between devices: 146 us -> 160 us
    all_gather x2 -> x0, blocking collectives: 78.5 us -> none  [forward_drive(): lax.all_gather(activity, 'cell', axis=1, tiled=True)]
    all_to_all x0 -> x2, starting transfers between devices: none -> 15.1 us  [forward_drive(): lax.all_to_all(jnp.stack([activity] * lax.axis_size('cell')), 'cell', 0, 0)]
    reduce_scatter x2, waiting for transfers between devices: 0.01 us -> 8.16 us  [forward_drive(): lax.psum_scatter(partial_rows, 'pre', scatter_dimension=1, tiled=True)]
    all_to_all x0 -> x2, waiting for transfers between devices: none -> 7.37 us  [forward_drive(): lax.all_to_all(jnp.stack([activity] * lax.axis_size('cell')), 'cell', 0, 0)]
  transfers between devices with their start and end apart: 4 -> 6, of which waited for: 2 -> 4; matrix products, arithmetic and copies ran while one was open for 11% -> 13% of each run, Pallas kernels for 0% -> 0%
where the time goes in v1:
time: 263 us; the launch traced here: 262 us
  waiting for transfers between devices  160 us (61%)
  other arithmetic  31.3 us (12%)
  local copies, waits for them, and re-layouts  21.8 us (8%)
  starting transfers between devices  15.4 us (6%)
  matrix products  15.3 us (6%)
  between operations  14 us (5%)
  blocking collectives  3.67 us (1%)
    reduce_scatter x2, waiting for transfers between devices, backward_drive(): lax.psum_scatter(partial_cols, 'cell', scatter_dimension=1, tiled=True)  145 us
    all_to_all x2, starting transfers between devices, forward_drive(): lax.all_to_all(jnp.stack([activity] * lax.axis_size('cell')), 'cell', 0, 0)  15.1 us
    another operation x3, other arithmetic, tree_inverse(): lower = jnp.linalg.cholesky(system)  12.4 us
    unnamed x30, local copies, waits for them, and re-layouts  10.8 us
    another operation x2, other arithmetic, tree_inverse(): lax.linalg.triangular_solve(lower, ident, left_side=True, lower=True)  10.5 us
    dot_general x4, matrix products, apply_matrix(): jnp.dot(matrix, field.reshape(depth, trials * cells), precision=lax.Preci...  10.4 us
    reduce_scatter x2, waiting for transfers between devices, forward_drive(): lax.psum_scatter(partial_rows, 'pre', scatter_dimension=1, tiled=True)  8.16 us
    dot_general x3, local copies, waits for them, and re-layouts, apply_matrix(): jnp.dot(matrix, field.reshape(depth, trials * cells), precision=lax.Preci...  7.75 us
  transfers between devices with their start and end apart: 6, of which 4 were waited for; matrix products, arithmetic and copies ran while one was open for 13% of the time, Pallas kernels for 0%

profile of v1, /device:TPU:0, one launch (start us, length us, event | category | flops | bytes accessed | tf_op | source)
XLA Modules:
  0.0 261.7 jit_solution(16319705810611774636)
XLA Ops:
  7.2 0.8 convert_bitcast_fusion
  8.6 8.3 %all-to-all-start = ((bf16[16,16,128]{2,1,0:T(8,128)(2,1)}), bf16[16,16,128]{2,1,0:T(8,128)(2,1)S(1)}, u32[]{:S(2)}, u32[]{:S(2)}) async-start(bf16[16,16,128]{2,1,0:T(8,128)(2,1)} %stack.7), calls=%async_computation | async-start | bytes 131072 | tf_op jit(solution)/shard_map/all_to_all | solution.py:33
  20.1 11.7 %cholesky.18 = f32[128,128]{1,0:T(8,128)S(1)} custom-call(f32[128,128]{1,0:T(8,128)S(1)} %fusion.24), custom_call_target="Cholesky" | custom-call | tf_op jit(solution)/shard_map/jit(cholesky)/cholesky | solution.py:19
  33.2 9.8 %custom-call.6 = f32[1,128,128]{1,2,0:T(8,128)S(1)} custom-call(f32[1,128,128]{2,1,0:T(8,128)S(1)} %fusion.8), custom_call_target="InvertDiagBlocksLowerTriangular" | custom-call | tf_op jit(solution)/shard_map/triangular_solve | solution.py:20
  43.6 1.0 fusion.12
  45.4 8.2 %reduce-scatter.5.cloned.1.call-done = f32[16,128]{1,0:T(8,128)} async-done(((f32[16,256]{1,0:T(8,128)}), f32[16,128]{1,0:T(8,128)}) %reduce-scatter.5.cloned.1.call-update) | async-done | bytes 8208 | tf_op jit(solution)/shard_map/reduce_scatter | solution.py:39
  53.6 1.1 fusion.1
  54.7 1.3 copy.55
  56.0 2.2 fusion.48
  59.0 6.7 %all-to-all-start.1 = ((bf16[16,16,128]{2,1,0:T(8,128)(2,1)}), bf16[16,16,128]{2,1,0:T(8,128)(2,1)S(1)}, u32[]{:S(2)}, u32[]{:S(2)}) async-start(bf16[16,16,128]{2,1,0:T(8,128)(2,1)} %stack.8), calls=%async_computation.2 | async-start | bytes 131072 | tf_op jit(solution)/shard_map/all_to_all | solution.py:33
  65.9 7.4 %all-to-all-done.1 = bf16[16,16,128]{2,1,0:T(8,128)(2,1)S(1)} async-done(((bf16[16,16,128]{2,1,0:T(8,128)(2,1)}), bf16[16,16,128]{2,1,0:T(8,128)(2,1)S(1)}, u32[]{:S(2)}, u32[]{:S(2)}) %all-to-all-start.1) | async-done | bytes 65568 | tf_op jit(solution)/shard_map/all_to_all | solution.py:33
  73.3 1.0 fusion.9
  74.6 2.5 copy.108
  77.1 2.6 copy.60
  80.8 2.9 %subtract_bitcast_fusion = (f32[16,16,8,128]{3,2,1,0:T(8,128)}, f32[2048,128]{0,1:T(8,128)}) fusion(f32[128,2048]{1,0:T(8,128)S(1)} %fusion.48, f32[2048]{0:T(1024)S(1)} %broadcast_bitcast_fusion, f32[16,8,16,128]{3,2,1,0:T(8,128)S(1)} %bitcast.135, f32[2048]{0:T(1024)S(1)} %bitcast.141, f32[16,8,16,128]{3,2,1,0:T(8,128)S(1)} %bitcast.137, ...), kind=kLoop, calls=%fused_computation.21 | loop fusion | flops 1835008 | bytes 6307840
  83.8 2.6 copy.73
  86.4 3.3 %fusion.7 = (bf16[16,128]{1,0:T(8,128)(2,1)S(1)}, f32[128,16,128]{2,0,1:T(8,128)}) fusion(f32[16,16,8,128]{3,2,1,0:T(8,128)} %get-tuple-element.34, f32[128,128]{1,0:T(8,128)S(1)} %fusion.35, f32[16,128,128]{2,1,0:T(8,128)S(1)} %bitcast.130, f32[128,128]{1,0:T(8,128)S(1)} %fusion.47), kind=kOutput, calls=%fused_computation.17 | convolution fusion | flops 403437568 | bytes 3280896 | tf_op jit(solution)/shard_map/dot_general | solution.py:26
  89.7 1.8 all_gather.6
  91.5 0.9 fusion.49
  92.5 1.9 multiply_subtract_fusion
  94.4 75.1 %reduce-scatter.9.cloned.1.call-done = f32[16,128]{1,0:T(8,128)} async-done(((f32[16,2048]{1,0:T(8,128)}), f32[16,128]{1,0:T(8,128)}) %reduce-scatter.9.cloned.1.call-update) | async-done | bytes 8208 | tf_op jit(solution)/shard_map/reduce_scatter | solution.py:48
  169.5 0.7 fusion.41
  170.2 1.3 copy.107
  171.5 2.5 copy.67
  174.0 2.6 %multiply_reduce_fusion = (bf16[16,128]{1,0:T(8,128)(2,1)S(1)}, f32[128,16,128]{2,0,1:T(8,128)S(1)}) fusion(f32[128,16,128]{2,1,0:T(8,128)S(1)} %copy-done.1, f32[128,128]{1,0:T(8,128)S(1)} %fusion.35, f32[16,128]{1,0:T(8,128)S(1)} %copy-done.3, f32[128,128]{1,0:T(8,128)S(1)} %broadcast_subtract_fusion, f32[16,128,128]{2,1,0:T(8,128)} %bitcast.131, ...), kind=kOutput, calls=%fused_computation.18 | convolution fusion | flops 404748288 | bytes 3354624 | tf_op jit(solution)/shard_map/dot_general | solution.py:26
  176.7 1.8 all_gather.7
  178.5 0.9 fusion.50
  179.5 2.2 fusion.19
  181.7 1.6 copy.69
  183.3 69.4 %reduce-scatter.11.cloned.1.call-done = f32[16,128]{1,0:T(8,128)} async-done(((f32[16,2048]{1,0:T(8,128)}), f32[16,128]{1,0:T(8,128)}) %reduce-scatter.11.cloned.1.call-update) | async-done | bytes 8208 | tf_op jit(solution)/shard_map/reduce_scatter | solution.py:48
  252.7 0.7 fusion.45
  253.5 1.6 copy.70
  (62 shorter events, 8.9 us)
Async XLA Ops:
  7.2 36.5 %copy-start = (bf16[256,2048]{1,0:T(8,128)(2,1)S(1)}, bf16[256,2048]{1,0:T(8,128)(2,1)}, u32[]{:S(2)}) copy-start(bf16[256,2048]{1,0:T(8,128)(2,1)} %param.17) | copy-start | bytes 3145732
  8.6 35.0 %all-to-all-start = ((bf16[16,16,128]{2,1,0:T(8,128)(2,1)}), bf16[16,16,128]{2,1,0:T(8,128)(2,1)S(1)}, u32[]{:S(2)}, u32[]{:S(2)}) async-start(bf16[16,16,128]{2,1,0:T(8,128)(2,1)} %stack.7), calls=%async_computation | async-start | bytes 131072 | tf_op jit(solution)/shard_map/all_to_all | solution.py:33
  17.0 0.7 copy-start.8
  17.0 36.6 %reduce-scatter.5.cloned.1.call-start = ((), (), s32[]{:S(2)}) async-start(), calls=%async_computation.6 | async-start | bytes 24576 | tf_op jit(solution)/shard_map/reduce_scatter | solution.py:39
  17.6 0.7 copy-start.9
  17.6 0.7 copy-start.12
  18.3 0.7 copy-start.10
  19.0 0.7 copy-start.11
  19.6 23.9 %copy-start.7 = (s32[2,16]{1,0:T(2,128)S(1)}, s32[2,16]{1,0:T(2,128)}, u32[]{:S(2)}) copy-start(s32[2,16]{1,0:T(2,128)} %param.25) | copy-start | bytes 388
  19.9 33.7 %copy-start.1 = (f32[128,16,128]{2,1,0:T(8,128)S(1)}, f32[128,16,128]{2,1,0:T(8,128)}, u32[]{:S(2)}) copy-start(f32[128,16,128]{2,1,0:T(8,128)} %param.15) | copy-start | bytes 3145732
  44.6 0.7 copy-start.5
  45.3 8.3 %copy-start.6 = (f32[128]{0:T(128)S(1)}, f32[128]{0:T(128)}, u32[]{:S(2)}) copy-start(f32[128]{0:T(128)} %param.19) | copy-start | bytes 1540
  59.0 14.3 %all-to-all-start.1 = ((bf16[16,16,128]{2,1,0:T(8,128)(2,1)}), bf16[16,16,128]{2,1,0:T(8,128)(2,1)S(1)}, u32[]{:S(2)}, u32[]{:S(2)}) async-start(bf16[16,16,128]{2,1,0:T(8,128)(2,1)} %stack.8), calls=%async_computation.2 | async-start | bytes 131072 | tf_op jit(solution)/shard_map/all_to_all | solution.py:33
  65.7 14.0 %reduce-scatter.7.cloned.1.call-start = ((), (), s32[]{:S(2)}) async-start(), calls=%async_computation.7 | async-start | bytes 24576 | tf_op jit(solution)/shard_map/reduce_scatter | solution.py:39
  74.3 95.2 %reduce-scatter.9.cloned.1.call-start = ((), (), s32[]{:S(2)}) async-start(), calls=%async_computation.8 | async-start | bytes 139264 | tf_op jit(solution)/shard_map/reduce_scatter | solution.py:48
  80.1 0.7 copy-start.4
  83.8 2.6 %copy-start.2 = (f32[2048,128]{1,0:T(8,128)S(1)}, f32[2048,128]{1,0:T(8,128)}, u32[]{:S(2)}) copy-start(f32[2048,128]{1,0:T(8,128)} %copy.60) | copy-start | bytes 3145732
  92.5 160.3 %reduce-scatter.11.cloned.1.call-start = ((), (), s32[]{:S(2)}) async-start(), calls=%async_computation.9 | async-start | bytes 139264 | tf_op jit(solution)/shard_map/reduce_scatter | solution.py:48
  171.5 2.5 copy-start.3
Sparse Core Ops, SparseCore 0:
  44.8 8.7 reduce-scatter.4
  74.4 4.2 reduce-scatter.6
  92.6 76.8 reduce-scatter.8
  179.6 73.1 reduce-scatter.10
